TPU v7x, 256 devices: a whole 4x4x8 slice. The times are simulated.
256 devices in a mesh: rep: 4 (over x_hi, core), fsdp: 64 (over x_lo, z, y).
Axes of the slice: x: 4 (x_hi: 2, x_lo: 2; x = x_hi * 2 + x_lo), y: 4, z: 8, core: 2. Of those that a mesh axis runs over, the one named last changes fastest.
Arguments:
- layer_inputs: bfloat16 [65536, 4608], P(('rep', 'fsdp')), may hold values from -24 to 24
- queries: bfloat16 [65536, 2048], P(('rep', 'fsdp')), may hold values from -32 to 32
- saved_keys: bfloat16 [65536, 1024], P(('rep', 'fsdp')), may hold values from -6 to 6
- saved_values: bfloat16 [65536, 1024], P(('rep', 'fsdp')), may hold values from -6 to 6
- out_grad: bfloat16 [65536, 2048], P(('rep', 'fsdp')), may hold values from -0.625 to 0.625
- global_params: float32 [4608, 1024], P('fsdp'), may hold values from -0.09375 to 0.09375
- replica_params: float32 [4, 4608, 1024], P('rep', 'fsdp'), may hold values from -0.09375 to 0.09375
- outer_momentum: float32 [4608, 1024], P('fsdp'), may hold values from -0.125 to 0.125
- next_inputs: bfloat16 [65536, 4608], P(('rep', 'fsdp')), may hold values from -6 to 6
Outputs:
- new_params: float32 [4608, 1024], P('fsdp')
- new_momentum: float32 [4608, 1024], P('fsdp')
- next_keys: bfloat16 [65536, 1024], P(('rep', 'fsdp'))
All inputs are finite; a program needn't handle non-finite values.
Results may differ from a plain program's by a relative error of at most 0.014.
Values may be sent and summed in bfloat16 or wider, within the bound.
A program may use at most 128 MiB of HBM per device.

v0:
```python
import jax
import jax.numpy as jnp
from jax import lax
from jax.sharding import Mesh
from jax.sharding import PartitionSpec as P

QH = 16
KVH = 8
HD = 128
FSDP = ("fsdp_0", "fsdp_1", "fsdp_2")
REP_FSDP = ("rep", "fsdp_0", "fsdp_1", "fsdp_2")


score_scale = 1.0 / 12.0
soft_cap = 50.0
rope_base = 10000.0
inner_rate = 0.02
outer_rate = 0.7
outer_beta = 0.9


def from_behind(block, axis, distance):
    devices = range(lax.axis_size(axis))
    route = [((i - distance) % len(devices), i) for i in devices]
    return lax.ppermute(block, axis, route)


def in_order(blocks, dim):
    blocks = jnp.moveaxis(blocks, 0, dim)
    lengths = blocks.shape
    return blocks.reshape(*lengths[:dim], lengths[dim] * lengths[dim + 1], *lengths[dim + 2 :])


def stacked_from(value, axes, turns):
    blocks = value
    for k in turns:
        blocks = lax.all_gather(blocks, axes[k])
    done = turns[::-1]
    back = [done.index(k) for k in range(len(axes))]
    blocks = blocks.transpose(*back, *range(len(axes), blocks.ndim))
    return blocks.reshape(-1, *value.shape)


def gather_axes(value, axes, turns, dim):
    return in_order(stacked_from(value, axes, turns), dim)


def rotate_back(grads, length):
    half = grads.shape[-1] // 2
    places = jnp.arange(length).astype(jnp.float32)
    freqs = rope_base ** (-jnp.arange(half).astype(jnp.float32) / half)
    angles = (places[:, None] * freqs[None, :])[:, None, :]
    cosine = jnp.cos(angles)
    sine = jnp.sin(angles)
    first = grads[..., :half]
    second = grads[..., half:]
    return jnp.concatenate(
        [first * cosine + second * sine, second * cosine - first * sine], axis=-1
    )


def attention_keys(query_rows, key_rows, value_rows, grad_rows):
    length = query_rows.shape[0]
    group = QH // KVH
    query_wide = query_rows.reshape(length, KVH, group, HD)
    key_wide = key_rows.reshape(length, KVH, HD)
    value_wide = value_rows.reshape(length, KVH, HD)
    grad_wide = grad_rows.reshape(length, KVH, group, HD)
    logits = (
        jnp.einsum("ihgd,jhd->hgij", query_wide, key_wide, preferred_element_type=jnp.float32)
        * score_scale
    )
    capped = jnp.tanh(logits / soft_cap)
    row_index = jnp.arange(length)
    causal = row_index[:, None] >= row_index[None, :]
    unnormed = jnp.where(causal, jnp.exp(soft_cap * capped), jnp.float32(0.0))
    probs = unnormed / jnp.sum(unnormed, axis=-1, keepdims=True)
    dprobs = jnp.einsum("ihgd,jhd->hgij", grad_wide, value_wide, preferred_element_type=jnp.float32)
    center = jnp.sum(probs * dprobs, axis=-1, keepdims=True)
    dlogits = (probs * (dprobs - center) * (1.0 - capped * capped) * score_scale).astype(
        jnp.bfloat16
    )
    rotated = jnp.einsum("hgij,ihgd->jhd", dlogits, query_wide, preferred_element_type=jnp.float32)
    plain = rotate_back(rotated, length)
    return plain.reshape(length, KVH * HD).astype(jnp.bfloat16)


def body(
    layer_inputs,
    queries,
    saved_keys,
    saved_values,
    out_grad,
    global_params,
    replica_params,
    outer_momentum,
    next_inputs,
):
    key_grad = attention_keys(queries, saved_keys, saved_values, out_grad)
    replicas = lax.axis_size("rep")
    own_local = replica_params[0]
    columns = layer_inputs
    group_grad = lax.psum_scatter(
        lax.dot_general(
            columns, key_grad, (((0,), (0,)), ((), ())), preferred_element_type=jnp.float32
        ),
        FSDP,
        scatter_dimension=0,
        tiled=True,
    )
    change = global_params - (own_local - inner_rate * group_grad)
    pieces = [change]
    moving = change
    for hop_index in range(1, replicas):
        moving = from_behind(moving, "rep", 1)
        pieces.append(moving)
    stacked = jnp.stack(pieces)
    order = (lax.axis_index("rep") - jnp.arange(replicas, dtype=jnp.int32)) % replicas
    summed = jnp.sum(jnp.take(stacked, order, axis=0), axis=0)
    outer_grad = summed / replicas
    fresh_momentum = outer_beta * outer_momentum + outer_grad
    fresh_params = global_params - outer_rate * (outer_grad + outer_beta * fresh_momentum)
    weights_low = fresh_params.astype(jnp.bfloat16)
    columns = next_inputs
    projected = jnp.dot(
        columns, gather_axes(weights_low, FSDP, (0, 1, 2), 0), preferred_element_type=jnp.float32
    )
    return (fresh_params, fresh_momentum, projected.astype(jnp.bfloat16))


def solution(mesh):
    finer = Mesh(
        mesh.devices.reshape(mesh.shape["rep"], 2, 8, 4), ("rep", "fsdp_0", "fsdp_1", "fsdp_2")
    )
    return jax.shard_map(
        body,
        mesh=finer,
        in_specs=(
            P(REP_FSDP, None),
            P(REP_FSDP, None),
            P(REP_FSDP, None),
            P(REP_FSDP, None),
            P(REP_FSDP, None),
            P(FSDP, None),
            P("rep", FSDP, None),
            P(FSDP, None),
            P(REP_FSDP, None),
        ),
        out_specs=(P(FSDP, None), P(FSDP, None), P(REP_FSDP, None)),
        check_vma=False,
    )
```

profile of v0, /device:TPU:1, one launch (start us, length us, event | category | flops | bytes accessed | tf_op | source)
XLA Modules:
  0.0 627.9 jit_solution(15274279776035495812)
XLA Ops:
  7.2 0.0 copy-start
  7.2 0.0 reduce-scatter.4.cloned.1.call-start
  7.3 1.6 copy.95
  8.9 1.1 copy.96
  10.1 0.0 copy-start.2
  10.1 0.8 copy-done.2
  10.9 2.7 fusion.18
  13.5 4.8 fusion.5
  18.3 2.6 reshape.139
  20.9 1.1 copy.97
  22.0 3.9 fusion.15
  25.9 0.3 multiply_cosine_fusion
  26.2 9.9 %fusion.13 = f32[256,8,128]{0,2,1:T(8,128)} fusion(bf16[256,8,2,128]{0,3,2,1:T(8,128)(2,1)S(1)} %bitcast.79, f32[8,2,256,256]{2,3,1,0:T(8,128)} %fusion.5, f32[8,256,256,2]{2,1,3,0:T(8,128)} %fusion.15, f32[8,256,256,2]{2,1,3,0:T(8,128)} %fusion.18), kind=kOutput, calls=%fused_computation.22 | convolution fusion | flops 277876992 | bytes 14680064 | tf_op jit(solution)/shard_map/hgij,ihgd->jhd/dot_general | solution.py:83
  36.2 1.3 add_convert_fusion
  37.6 0.0 copy-done
  37.6 7.9 %convolution_bitcast_fusion = f32[4608,1024]{0,1:T(8,128)} fusion(bf16[256,1024]{0,1:T(8,128)(2,1)S(1)} %bitcast.80, bf16[256,4608]{1,0:T(8,128)(2,1)S(1)} %copy-done), kind=kOutput, calls=%fused_computation.3 | convolution fusion | flops 2415919104 | bytes 21757952 | tf_op jit(solution)/shard_map/dot_general | solution.py:104
  45.4 18.6 %copy.93 = f32[4608,1024]{1,0:T(8,128)} copy(f32[4608,1024]{0,1:T(8,128)} %convolution_bitcast_fusion) | data formatting | bytes 37748736
  64.1 0.0 copy-start.6
  64.1 0.0 copy-start.7
  64.1 0.0 reduce-scatter.4.cloned.1.call-update
  64.1 0.0 all-gather.6.cloned.1.call-start
  64.2 0.9 copy-done.6
  65.0 0.2 copy.79
  65.2 0.0 copy-done.7
  65.2 0.2 copy.70
  65.4 317.2 %reduce-scatter.4.cloned.1.call-done = f32[72,1024]{1,0:T(8,128)} async-done(((f32[4608,1024]{1,0:T(8,128)}), f32[72,1024]{1,0:T(8,128)}) %reduce-scatter.4.cloned.1.call-update) | async-done | bytes 294928
  382.7 1.2 copy.94
  383.8 0.1 fusion.20
  383.9 0.0 copy-start.3
  383.9 50.5 %collective-permute-start = (f32[72,1024]{0,1:T(8,128)S(1)}, f32[72,1024]{0,1:T(8,128)S(1)}, u32[]{:S(2)}, u32[]{:S(2)}) collective-permute-start(f32[72,1024]{0,1:T(8,128)S(1)} %fusion.20), channel_id=1, source_target_pairs={{192,0},{0,64},{64,128},{128,192},{193,1},{1,65},{65,129},{129,193... | collective-permute-start | bytes 884744 | tf_op jit(solution)/shard_map/ppermute | solution.py:25
  434.4 6.1 collective-permute-done
  440.6 0.0 copy-start.4
  440.6 4.0 collective-permute-start.1
  444.5 1.2 copy.78
  445.7 5.0 collective-permute-done.1
  450.7 0.0 copy-start.5
  450.7 4.0 collective-permute-start.2
  454.7 6.1 collective-permute-done.2
  460.8 0.0 copy-done.3
  460.8 0.0 copy-done.4
  460.8 0.0 copy-done.5
  460.8 1.5 pad_maximum_fusion
  462.3 2.0 gather_fusion
  464.3 1.9 select_reduce_fusion
  466.2 0.2 fusion.35
  466.4 0.1 copy.80
  466.5 5.3 all-gather
  471.9 0.0 all-gather.6.cloned.1.call-update
  471.9 0.2 all-gather.8.cloned.1.call-start
  472.1 33.6 %all-gather.6.cloned.1.call-done = bf16[16,72,1024]{2,1,0:T(8,128)(2,1)} async-done(((bf16[2,72,1024]{2,1,0:T(8,128)(2,1)}), bf16[16,72,1024]{2,1,0:T(8,128)(2,1)}) %all-gather.6.cloned.1.call-update) | async-done | bytes 2359312 | tf_op jit(solution)/shard_map/all_gather | solution.py:37
  505.7 0.0 all-gather.8.cloned.1.call-update
  505.7 0.9 copy.82
  506.6 0.9 copy.83
  507.5 96.7 %all-gather.8.cloned.1.call-done = bf16[32,2,72,1024]{3,2,1,0:T(8,128)(2,1)} async-done(((bf16[8,2,72,1024]{3,2,1,0:T(8,128)(2,1)}), bf16[32,2,72,1024]{3,2,1,0:T(8,128)(2,1)}) %all-gather.8.cloned.1.call-update) | async-done | bytes 9437200 | tf_op jit(solution)/shard_map/all_gather | solution.py:37
  604.3 9.0 %copy.81 = bf16[2,8,4,72,1024]{4,3,2,1,0:T(8,128)(2,1)} copy(bf16[2,8,4,72,1024]{4,3,0,1,2:T(8,128)(2,1)} %bitcast.75) | data formatting | bytes 18874368 | tf_op jit(solution)/shard_map/transpose | solution.py:40
  613.2 0.0 copy-start.1
  613.3 7.1 %fusion.14 = bf16[256,1024]{0,1:T(8,128)(2,1)S(1)} fusion(bf16[4608,1024]{1,0:T(8,128)(2,1)} %bitcast.76, bf16[256,4608]{1,0:T(8,128)(2,1)} %param.17), kind=kOutput, calls=%fused_computation.24 | convolution fusion | flops 2416181248 | bytes 12320768 | tf_op jit(solution)/shard_map/dot_general | solution.py:125
  620.4 1.0 copy.84
  621.4 0.0 copy-done.1
  (7 shorter events, 0.1 us)
Async XLA Ops:
  7.2 30.4 %copy-start = (bf16[256,4608]{1,0:T(8,128)(2,1)S(1)}, bf16[256,4608]{1,0:T(8,128)(2,1)}, u32[]{:S(2)}) copy-start(bf16[256,4608]{1,0:T(8,128)(2,1)} %param.9) | copy-start | bytes 7077892
  7.2 375.5 %reduce-scatter.4.cloned.1.call-start = ((), (), s32[]{:S(2)}) async-start(), calls=%async_computation.3 | async-start | bytes 19169280
  10.1 0.8 copy-start.2
  64.1 1.0 copy-start.6
  64.1 1.2 copy-start.7
  64.1 441.6 %all-gather.6.cloned.1.call-start = ((), (), s32[]{:S(2)}) async-start(), calls=%async_computation.1 | async-start | bytes 2654208 | tf_op jit(solution)/shard_map/all_gather | solution.py:37
  383.9 76.9 %copy-start.3 = (f32[72,1024]{0,1:T(8,128)}, f32[72,1024]{0,1:T(8,128)S(1)}, u32[]{:S(2)}) copy-start(f32[72,1024]{0,1:T(8,128)S(1)} %fusion.20) | copy-start | bytes 884740
  383.9 56.6 %collective-permute-start = (f32[72,1024]{0,1:T(8,128)S(1)}, f32[72,1024]{0,1:T(8,128)S(1)}, u32[]{:S(2)}, u32[]{:S(2)}) collective-permute-start(f32[72,1024]{0,1:T(8,128)S(1)} %fusion.20), channel_id=1, source_target_pairs={{192,0},{0,64},{64,128},{128,192},{193,1},{1,65},{65,129},{129,193... | collective-permute-start | bytes 884744 | tf_op jit(solution)/shard_map/ppermute | solution.py:25
  440.6 20.2 %copy-start.4 = (f32[72,1024]{0,1:T(8,128)}, f32[72,1024]{0,1:T(8,128)S(1)}, u32[]{:S(2)}) copy-start(f32[72,1024]{0,1:T(8,128)S(1)} %collective-permute-done) | copy-start | bytes 884740
  440.6 10.1 %collective-permute-start.1 = (f32[72,1024]{0,1:T(8,128)S(1)}, f32[72,1024]{0,1:T(8,128)S(1)}, u32[]{:S(2)}, u32[]{:S(2)}) collective-permute-start(f32[72,1024]{0,1:T(8,128)S(1)} %collective-permute-done), channel_id=1, source_target_pairs={{192,0},{0,64},{64,128},{128,192},{193,1},{1,65},{65,129},{129,193... | collective-permute-start | bytes 884744 | tf_op jit(solution)/shard_map/ppermute | solution.py:25
  450.7 10.1 %copy-start.5 = (f32[72,1024]{0,1:T(8,128)}, f32[72,1024]{0,1:T(8,128)S(1)}, u32[]{:S(2)}) copy-start(f32[72,1024]{0,1:T(8,128)S(1)} %collective-permute-done.1) | copy-start | bytes 884740
  450.7 10.1 %collective-permute-start.2 = (f32[72,1024]{0,1:T(8,128)S(1)}, f32[72,1024]{0,1:T(8,128)S(1)}, u32[]{:S(2)}, u32[]{:S(2)}) collective-permute-start(f32[72,1024]{0,1:T(8,128)S(1)} %collective-permute-done.1), channel_id=1, source_target_pairs={{192,0},{0,64},{64,128},{128,192},{193,1},{1,65},{65,129},{129,193... | collective-permute-start | bytes 884744 | tf_op jit(solution)/shard_map/ppermute | solution.py:25
  471.9 132.4 %all-gather.8.cloned.1.call-start = ((), (), s32[]{:S(2)}) async-start(), calls=%async_computation.2 | async-start | bytes 11796480 | tf_op jit(solution)/shard_map/all_gather | solution.py:37
  613.2 8.1 %copy-start.1 = (bf16[256,4608]{1,0:T(8,128)(2,1)S(1)}, bf16[256,4608]{1,0:T(8,128)(2,1)}, u32[]{:S(2)}) copy-start(bf16[256,4608]{1,0:T(8,128)(2,1)} %param.9) | copy-start | bytes 7077892
Sparse Core Ops, SparseCore 0:
  64.2 318.3 reduce-scatter.3
  472.0 33.6 all-gather.5
  507.5 96.7 all-gather.7
where the time goes:
time: 629 us; the launch traced here: 628 us
  waiting for transfers between devices  465 us (74%)
  starting transfers between devices  58.8 us (9%)
  local copies, waits for them, and re-layouts  43.4 us (7%)
  matrix products  36.3 us (6%)
  between operations  13.9 us (2%)
    unnamed x4, waiting for transfers between devices  317 us
    all_gather x2, waiting for transfers between devices, stacked_from(): blocks = lax.all_gather(blocks, axes[k])  130 us
    ppermute x3, starting transfers between devices, from_behind(): return lax.ppermute(block, axis, route)  58.5 us
    unnamed x26, local copies, waits for them, and re-layouts  28.1 us
    ppermute x3, waiting for transfers between devices, from_behind(): return lax.ppermute(block, axis, route)  17.2 us
  transfers between devices with their start and end apart: 6, of which 6 were waited for; matrix products, arithmetic and copies ran while one was open for 1% of the time, Pallas kernels for 0%

commit v1 on v0

v1 whole, which is shorter than its diff:
```python
import jax
import jax.numpy as jnp
import numpy as np
from jax import lax
from jax.experimental import pallas as pl
from jax.experimental.pallas import tpu as pltpu
from jax.sharding import PartitionSpec as P

MESH = pl.DeviceIdType.MESH
BF16 = jnp.bfloat16
F32 = jnp.float32

HD = 128
KVH = 8
SEQ = 256
D = 4608
SHARD = 72
THIRD = 24
PORTIONS = 6
STEPS = 7
score_scale = 1.0 / 12.0
soft_cap = 50.0
rope_base = 10000.0
inner_rate = 0.02
outer_rate = 0.7
outer_beta = 0.9

CUBE = ("xa", "ya", "za", "xb", "yb", "zb")


def order_of(k):
    return tuple(CUBE[(k + j) % 6] for j in range(6)) + ("zc",)


def bits_of(x_hi, x_lo, z, y):
    return {
        "xa": (x_hi + x_lo) % 2,
        "xb": x_hi,
        "ya": (y + y // 2) % 2,
        "yb": y // 2,
        "za": (z + z // 2) % 2,
        "zb": (z // 2) % 2,
        "zc": z // 4,
    }


def place_of(bits, k):
    place = 0
    for name in order_of(k):
        place = place * 2 + bits[name]
    return place


def partner_of(name, x_hi, x_lo, z, y):
    if name == "xa":
        return x_hi, 1 - x_lo, z, y
    if name == "xb":
        return 1 - x_hi, 1 - x_lo, z, y
    if name == "ya":
        return x_hi, x_lo, z, y + 1 - 2 * (y % 2)
    if name == "yb":
        return x_hi, x_lo, z, 3 - y
    if name == "za":
        return x_hi, x_lo, z + 1 - 2 * (z % 2), y
    if name == "zb":
        return x_hi, x_lo, (z + 7 + 2 * (z % 2)) % 8, y
    return x_hi, x_lo, (z + 4) % 8, y


def kernel(
    x_ref, q_ref, k_ref, v_ref, g_ref, gp_ref, rp_ref, om_ref, cos_ref, sin_ref, ni_ref,
    np_ref, nm_ref, nk_ref,
    xt, kg, kg_sib, grad, recv, weights, w_full, ni, changes, og, o_send, o_recv,
    rs_send, rs_recv, ag_send, ag_recv, rep_send, rep_recv, og_send, og_recv,
    ni_sem, ni_send, ni_recv, xt_send, xt_recv, kg_send, kg_recv, o_ssem, o_rsem,
):
    rep = lax.axis_index("rep")
    fsdp = lax.axis_index("fsdp")
    x_hi, core = rep // 2, rep % 2
    x_lo, z, y = fsdp // 32, (fsdp // 4) % 8, fsdp % 4

    def device(x_hi, x_lo, z, y, core):
        return (x_hi * 2 + core, (x_lo * 8 + z) * 4 + y)

    sibling = device(x_hi, x_lo, z, y, 1 - core)
    partner = {
        name: device(*partner_of(name, x_hi, x_lo, z, y), core) for name in CUBE + ("zc",)
    }
    rep_peers = [
        (x_hi, 1 - core, sibling),
        (1 - x_hi, core, device(1 - x_hi, x_lo, z, y, core)),
        (1 - x_hi, 1 - core, device(1 - x_hi, x_lo, z, y, 1 - core)),
    ]

    barrier = pltpu.get_barrier_semaphore()
    peers = [sibling] + [partner[name] for name in CUBE + ("zc",)] + [rep_peers[1][2], rep_peers[2][2]]
    for peer in peers:
        pl.semaphore_signal(barrier, inc=1, device_id=peer, device_id_type=MESH)
    pl.semaphore_wait(barrier, len(peers))

    def remote(src, dst, send, receive, peer):
        return pltpu.make_async_remote_copy(
            src_ref=src, dst_ref=dst, send_sem=send, recv_sem=receive, device_id=peer, device_id_type=MESH
        )

    rep_copies = []
    for i, (p_hi, p_core, peer) in enumerate(rep_peers):
        block = pl.ds(pl.multiple_of((p_core * 2 + p_hi) * 256, 256), 256)
        copy = remote(rp_ref.at[:, block], changes.at[i], rep_send.at[i], rep_recv.at[i], peer)
        copy.start()
        rep_copies.append(copy)

    def turn(c, _):
        cols = pl.ds(pl.multiple_of(c * 1152, 1152), 1152)
        xt[pl.ds(pl.multiple_of(c * 1152, 1152), 1152), 0:256] = x_ref[:, cols].T
        return 0

    lax.fori_loop(0, 4, turn, 0)
    xt_copy = remote(xt.at[:, 0:256], xt.at[:, 256:512], xt_send, xt_recv, sibling)
    xt_copy.start()
    ni_local = pltpu.make_async_copy(ni_ref, ni.at[0], ni_sem)
    ni_local.start()
    ni_copy = remote(ni_ref, ni.at[1], ni_send, ni_recv, sibling)
    ni_copy.start()

    nt = (((1,), (1,)), ((), ()))

    def head(h, _):
        lanes = pl.ds(pl.multiple_of(h * HD, HD), HD)
        keys = k_ref[:, lanes]
        values = v_ref[:, lanes]
        low = jnp.zeros((128, HD), F32)
        high = jnp.zeros((128, HD), F32)
        for g in range(2):
            wide = pl.ds(pl.multiple_of(h * 256 + g * HD, HD), HD)
            for b in range(2):
                rows = slice(b * 128, b * 128 + 128)
                n = (b + 1) * 128
                qb = q_ref[rows, wide]
                gb = g_ref[rows, wide]
                logits = lax.dot_general(keys[:n], qb, nt, preferred_element_type=F32)
                dprobs = lax.dot_general(values[:n], gb, nt, preferred_element_type=F32)
                capped = jnp.tanh(logits * (score_scale / soft_cap))
                unnormed = jnp.exp(soft_cap * capped)
                key_at = lax.broadcasted_iota(jnp.int32, (n, 128), 0)
                query_at = lax.broadcasted_iota(jnp.int32, (n, 128), 1) + b * 128
                unnormed = jnp.where(query_at >= key_at, unnormed, 0.0)
                inverse = 1.0 / jnp.sum(unnormed, axis=0, keepdims=True)
                center = jnp.sum(unnormed * dprobs, axis=0, keepdims=True) * inverse
                dlogits = (
                    unnormed * (dprobs - center) * ((1.0 - capped * capped) * (inverse * score_scale))
                ).astype(BF16)
                part = jnp.dot(dlogits, qb, preferred_element_type=F32)
                low = low + part[:128]
                if b == 1:
                    high = high + part[128:]
        half, x_part, ch = h // 4, (h // 2) % 2, h % 2
        out_lanes = pl.ds(pl.multiple_of(x_part * HD, HD), HD)
        for b, rotated in ((0, low), (1, high)):
            rows = slice(b * 128, b * 128 + 128)
            plain = rotated * cos_ref[rows, :] + pltpu.roll(rotated, 64, 1) * sin_ref[rows, :]
            kg[half, ch, rows, out_lanes] = plain.astype(BF16)
        return 0

    lax.fori_loop(0, KVH, head, 0)

    kg_copy = remote(kg.at[1 - core], kg_sib, kg_send, kg_recv, sibling)
    kg_copy.start()
    xt_copy.wait_recv()
    kg_copy.wait_recv()

    mine = bits_of(x_hi, x_lo, z, y)

    def start_of(k, j, flip):
        place = 0
        for name in order_of(k)[:j]:
            place = place * 2 + mine[name]
        last = mine[order_of(k)[j]]
        place = place * 2 + (1 - last if flip else last)
        return place * 2 ** (6 - j)

    def rs_copy(k, j):
        n = 2 ** (6 - j)
        return remote(
            grad.at[k, pl.ds(start_of(k, j, True), n)],
            recv.at[k, pl.ds(128 - 2 * n, n)],
            rs_send.at[k, j],
            rs_recv.at[k, j],
            partner[order_of(k)[j]],
        )

    for ch in range(2):
        def quarter(c, _, ch=ch):
            rows = pl.ds(pl.multiple_of(c * 1152, 1152), 1152)
            part = jnp.dot(
                xt[rows, 0:256], kg[core, ch], preferred_element_type=F32
            ) + jnp.dot(xt[rows, 256:512], kg_sib[ch], preferred_element_type=F32)
            for i in range(16):
                for t_hi in range(2):
                    bits = bits_of(t_hi, c // 2, i // 4, i % 4)
                    bits["zc"] = c % 2
                    for third in range(3):
                        k = ch * 3 + third
                        row = i * SHARD + third * THIRD
                        piece = part[row : row + THIRD, t_hi * 128 : t_hi * 128 + 128]
                        grad[k, place_of(bits, k)] = piece.astype(BF16)
            return 0

        lax.fori_loop(0, 4, quarter, 0)
        for third in range(3):
            rs_copy(ch * 3 + third, 0).start()

    for j in range(STEPS):
        n = 2 ** (6 - j)
        m = min(n, 8)
        for k in range(PORTIONS):
            rs_copy(k, j).wait_recv()
            base = start_of(k, j, False)

            def add(i, _, k=k, n=n, m=m, base=base):
                here = pl.ds(base + i * m, m)
                grad[k, here] = grad[k, here] + recv[k, pl.ds(128 - 2 * n + i * m, m)]
                return 0

            if n == m:
                add(0, 0)
            else:
                lax.fori_loop(0, n // m, add, 0)
            if j + 1 < STEPS:
                rs_copy(k, j + 1).start()

    for copy in rep_copies:
        copy.wait_recv()
    own = core * 2 + x_hi
    for ch in range(2):
        cols = pl.ds(pl.multiple_of(own * 256 + ch * 128, 128), 128)
        lanes = slice(ch * 128, ch * 128 + 128)
        for third in range(3):
            k = ch * 3 + third
            rows = slice(third * THIRD, third * THIRD + THIRD)
            place = start_of(k, 6, False)
            before = gp_ref[rows, cols]
            moved = before - rp_ref[rows, cols]
            for i in range(3):
                moved = moved + (before - changes[i, rows, lanes])
            outer = (moved + inner_rate * grad[k, place].astype(F32)) * 0.25
            og[own, rows, lanes] = outer
            fresh = outer_beta * om_ref[rows, cols] + outer
            weights[k, place] = (before - outer_rate * (outer + outer_beta * fresh)).astype(BF16)

    def ag_copy(k, j):
        n = 2 ** (6 - j)
        here = pl.ds(start_of(k, j, False), n)
        return remote(
            weights.at[k, here], weights.at[k, here], ag_send.at[k, j], ag_recv.at[k, j], partner[order_of(k)[j]]
        )

    for k in range(PORTIONS):
        ag_copy(k, 6).start()
    for j in range(6, 0, -1):
        for k in range(PORTIONS):
            ag_copy(k, j).wait_recv()
            ag_copy(k, j - 1).start()
    og_copies = []
    for i, (_, _, peer) in enumerate(rep_peers):
        copy = remote(og.at[own], og.at[own], og_send.at[i], og_recv.at[i], peer)
        copy.start()
        og_copies.append(copy)
    for k in range(PORTIONS):
        ag_copy(k, 0).wait_recv()

    def place_rows(c, _):
        for i in range(16):
            for t_hi in range(2):
                bits = bits_of(t_hi, c // 2, i // 4, i % 4)
                bits["zc"] = c % 2
                for k in range(PORTIONS):
                    ch, third = k // 3, k % 3
                    row = i * SHARD + third * THIRD
                    lane = t_hi * 256 + ch * 128
                    w_full[c, row : row + THIRD, lane : lane + 128] = weights[k, place_of(bits, k)]
        return 0

    lax.fori_loop(0, 4, place_rows, 0)
    ni_local.wait()
    ni_copy.wait_recv()

    def project(side):
        total = jnp.zeros((SEQ, 512), F32)
        for part in range(2):
            total = total + jnp.dot(
                ni[side, :, part * 2304 : part * 2304 + 2304],
                w_full[2 * part : 2 * part + 2].reshape(2304, 512),
                preferred_element_type=F32,
            )
        return total.astype(BF16)

    o_send[...] = project(1)
    o_copy = remote(o_send, o_recv, o_ssem, o_rsem, sibling)
    o_copy.start()
    nk_ref[:, pl.ds(pl.multiple_of(core * 512, 512), 512)] = project(0)

    for copy in og_copies:
        copy.wait_recv()
    for b in range(4):
        lanes = slice(b * 256, b * 256 + 256)
        outer = og[b]
        fresh = outer_beta * om_ref[:, lanes] + outer
        nm_ref[:, lanes] = fresh
        np_ref[:, lanes] = gp_ref[:, lanes] - outer_rate * (outer + outer_beta * fresh)
    o_copy.wait_recv()
    nk_ref[:, pl.ds(pl.multiple_of((1 - core) * 512, 512), 512)] = o_recv[...]

    for k in range(PORTIONS):
        for j in range(STEPS):
            rs_copy(k, j).wait_send()
            ag_copy(k, j).wait_send()
    for copy in rep_copies + og_copies + [xt_copy, ni_copy, kg_copy, o_copy]:
        copy.wait_send()


def turning():
    half = HD // 2
    freqs = np.float32(rope_base) ** (-np.arange(half, dtype=np.float32) / np.float32(half))
    angles = np.arange(SEQ, dtype=np.float32)[:, None] * freqs[None, :].astype(np.float32)
    cosine, sine = np.cos(angles), np.sin(angles)
    return (
        np.concatenate([cosine, cosine], axis=1).astype(np.float32),
        np.concatenate([sine, -sine], axis=1).astype(np.float32),
    )


def body(layer_inputs, queries, saved_keys, saved_values, out_grad, global_params, replica_params, outer_momentum, next_inputs):
    cosine, sine = turning()
    vmem = pl.BlockSpec(memory_space=pltpu.VMEM)
    dma = pltpu.SemaphoreType.DMA
    return pl.pallas_call(
        kernel,
        out_shape=(
            jax.ShapeDtypeStruct((SHARD, 1024), F32),
            jax.ShapeDtypeStruct((SHARD, 1024), F32),
            jax.ShapeDtypeStruct((SEQ, 1024), BF16),
        ),
        in_specs=[vmem] * 10 + [pl.BlockSpec(memory_space=pl.ANY)],
        out_specs=(vmem, vmem, vmem),
        scratch_shapes=[
            pltpu.VMEM((D, 512), BF16),
            pltpu.VMEM((2, 2, SEQ, 256), BF16),
            pltpu.VMEM((2, SEQ, 256), BF16),
            pltpu.VMEM((PORTIONS, 128, THIRD, 128), BF16),
            pltpu.VMEM((PORTIONS, 128, THIRD, 128), BF16),
            pltpu.VMEM((PORTIONS, 128, THIRD, 128), BF16),
            pltpu.VMEM((4, 1152, 512), BF16),
            pltpu.VMEM((2, SEQ, D), BF16),
            pltpu.VMEM((3, SHARD, 256), F32),
            pltpu.VMEM((4, SHARD, 256), F32),
            pltpu.VMEM((SEQ, 512), BF16),
            pltpu.VMEM((SEQ, 512), BF16),
            dma((PORTIONS, STEPS)),
            dma((PORTIONS, STEPS)),
            dma((PORTIONS, STEPS)),
            dma((PORTIONS, STEPS)),
            dma((3,)),
            dma((3,)),
            dma((3,)),
            dma((3,)),
        ]
        + [dma] * 9,
        compiler_params=pltpu.CompilerParams(
            collective_id=0, has_side_effects=True, vmem_limit_bytes=60 * 1024 * 1024
        ),
    )(
        layer_inputs, queries, saved_keys, saved_values, out_grad, global_params, replica_params[0],
        outer_momentum, cosine, sine, next_inputs,
    )


def solution(mesh):
    both = ("rep", "fsdp")
    return jax.shard_map(
        body,
        mesh=mesh,
        in_specs=(
            P(both, None), P(both, None), P(both, None), P(both, None), P(both, None),
            P("fsdp", None), P("rep", "fsdp", None), P("fsdp", None), P(both, None),
        ),
        out_specs=(P("fsdp", None), P("fsdp", None), P(both, None)),
        check_vma=False,
    )
```

time: 629 us -> 112 us (0.18)
  waiting for transfers between devices: 465 us -> 0 us
  Pallas kernels: 0 us -> 106 us
  starting transfers between devices: 58.8 us -> 0 us
  local copies, waits for them, and re-layouts: 43.4 us -> 5.26 us
  matrix products: 36.3 us -> 0 us
  between operations: 13.9 us -> 0.64 us
    unnamed x4 -> x0, waiting for transfers between devices: 317 us -> none
    all_gather x2 -> x0, waiting for transfers between devices: 130 us -> none  [stacked_from(): blocks = lax.all_gather(blocks, axes[k])]
    pallas_call x0 -> x1, Pallas kernels: none -> 106 us  [body(): pl.pallas_call(kernel, out_shape=(jax.ShapeDtypeStruct((SHARD, 1024), F32...]
    ppermute x3 -> x0, starting transfers between devices: 58.5 us -> none  [from_behind(): return lax.ppermute(block, axis, route)]
    dot_general x5 -> x0, matrix products: 31.5 us -> none  [the longest x1 9.94 us: attention_keys(): jnp.einsum('hgij,ihgd->jhd', dlogits, query_wide, preferred_element_type=...]
    unnamed x26 -> x3, local copies, waits for them, and re-layouts: 28.1 us -> 5.26 us
    ppermute x3 -> x0, waiting for transfers between devices: 17.2 us -> none  [from_behind(): return lax.ppermute(block, axis, route)]
    transpose x1 -> x0, local copies, waits for them, and re-layouts: 8.97 us -> none  [stacked_from(): blocks = blocks.transpose(*back, *range(len(axes), blocks.ndim))]
  transfers between devices with their start and end apart: 6 -> 0, of which waited for: 6 -> 0; matrix products, arithmetic and copies ran while one was open for 1% -> 0% of each run, Pallas kernels for 0% -> 0%
where the time goes in v1:
time: 112 us
  Pallas kernels  106 us (95%)
  local copies, waits for them, and re-layouts  5.26 us (5%)
    pallas_call x1, Pallas kernels, body(): pl.pallas_call(kernel, out_shape=(jax.ShapeDtypeStruct((SHARD, 1024), F32...  106 us
    unnamed x3, local copies, waits for them, and re-layouts  5.26 us

profile of v1, /device:TPU:1, one launch (start us, length us, event | category | flops | bytes accessed | tf_op | source)
XLA Modules:
  0.0 111.7 jit_solution(16943433886933686994)
XLA Ops:
  0.6 105.8 %shard_map.130 = (f32[72,1024]{1,0:T(8,128)}, f32[72,1024]{1,0:T(8,128)}, bf16[256,1024]{1,0:T(8,128)(2,1)}) custom-call(bf16[256,4608]{1,0:T(8,128)(2,1)} %x_ref.1, bf16[256,2048]{1,0:T(8,128)(2,1)} %q_ref.1, bf16[256,1024]{1,0:T(8,128)(2,1)} %k_ref.1, bf16[256,1024]{1,0:T(8,128)(2,1)} %v_ref.1, bf16[256,2048]{1,0:T(8,128)(2,1)} %g_ref.1, ...), custom_call_target="tpu_custom_call" | custom-call | tf_op jit(solution)/shard_map/pallas_call | solution.py:337
  106.4 1.7 %copy.17 = f32[72,1024]{1,0:T(8,128)} copy(f32[72,1024]{1,0:T(8,128)} %get-tuple-element.6) | data formatting | bytes 589824
  108.1 1.7 %copy.18 = f32[72,1024]{1,0:T(8,128)} copy(f32[72,1024]{1,0:T(8,128)} %get-tuple-element.7) | data formatting | bytes 589824
  109.8 1.9 %copy.19 = bf16[256,1024]{1,0:T(8,128)(2,1)} copy(bf16[256,1024]{1,0:T(8,128)(2,1)} %get-tuple-element.8) | data formatting | bytes 1048576

commit v2 on v1

v2 whole, which is shorter than its diff:
```python
import contextlib

import jax
import jax.numpy as jnp
import numpy as np
from jax import lax
from jax.experimental import pallas as pl
from jax.experimental.pallas import tpu as pltpu
from jax.sharding import PartitionSpec as P

MESH = pl.DeviceIdType.MESH
BF16 = jnp.bfloat16
F32 = jnp.float32

HD = 128
SEQ = 256
D = 4608
SHARD = 72
PORTIONS = 6
SUBS = 3
score_scale = 1.0 / 12.0
soft_cap = 50.0
rope_base = 10000.0
inner_rate = 0.02
outer_rate = 0.7
outer_beta = 0.9

CUBE = ("xa", "ya", "za", "xb", "yb", "zb")


def order_of(k):
    return tuple(CUBE[(k + j) % 6] for j in range(6)) + ("zc",)


def later_z(k):
    return order_of(k).index("zb") < order_of(k).index("za")


def z_bits(hi, lo):
    third = (hi + (lo + 1) // 4) % 2
    return (lo + lo // 2) % 2, (lo // 2 + third) % 2, third


def bits_of(k, x_hi, x_lo, z_hi, z_lo, y):
    bits = {"xa": (x_hi + x_lo) % 2, "xb": x_hi, "ya": (y + y // 2) % 2, "yb": y // 2}
    if later_z(k):
        if isinstance(z_lo, int):
            hi, lo = (z_hi, z_lo - 1) if z_lo else (z_hi + 1, 3)
        else:
            before = (z_hi * 4 + z_lo + 7) % 8
            hi, lo = before // 4, before % 4
        bits["zb"], bits["za"], bits["zc"] = z_bits(hi, lo)
    else:
        bits["za"], bits["zb"], bits["zc"] = z_bits(z_hi, z_lo)
    return bits


def place_of(bits, k):
    place = 0
    for name in order_of(k):
        place = place * 2 + bits[name]
    return place


def partner_of(k, name, x_hi, x_lo, z, y):
    if name == "xa":
        return x_hi, 1 - x_lo, z, y
    if name == "xb":
        return 1 - x_hi, 1 - x_lo, z, y
    if name == "ya":
        return x_hi, x_lo, z, y + 1 - 2 * (y % 2)
    if name == "yb":
        return x_hi, x_lo, z, 3 - y
    if name == "za":
        return x_hi, x_lo, z + 1 - 2 * (z % 2), y
    if name == "zb":
        return x_hi, x_lo, (z + 7 + 2 * (z % 2)) % 8, y
    if later_z(k):
        return x_hi, x_lo, (z + 5 - 2 * (z % 2)) % 8, y
    return x_hi, x_lo, (z + 3 + 2 * (z % 2)) % 8, y


def tile_of(k, s):
    return (s * PORTIONS + k) // 9, (s * PORTIONS + k) % 9


def kernel(
    x_hbm, q_hbm, k_hbm, v_hbm, g_hbm, gp_hbm, rp_hbm, om_hbm, cos_hbm, sin_hbm, ni_hbm,
    np_ref, nm_ref, nk_ref,
    x_ref, q_ref, k_ref, v_ref, g_ref, gp_ref, rp_ref, om_ref, cos_ref, sin_ref, ni,
    xt, kg, kg_sib, grad, recv, n_keep, n_recv, n_sum, n_recv2, n_w, weights, w_full, changes, og, o_send, o_recv,
    in_sem, rs_send, rs_recv, r2_send, r2_recv, keep_send, keep_recv, n_rs_send, n_rs_recv, n_ag_send, n_ag_recv,
    a2_send, a2_recv, own_send, own_recv, ag_send, ag_recv, rep_send, rep_recv, og_send, og_recv,
    ni_send, ni_recv, xt_send, xt_recv, kg_send, kg_recv, o_ssem, o_rsem,
):
    rep = lax.axis_index("rep")
    fsdp = lax.axis_index("fsdp")
    x_hi, core = rep // 2, rep % 2
    x_lo, z, y = fsdp // 32, (fsdp // 4) % 8, fsdp % 4
    portions = range(PORTIONS)

    def device(x_hi, x_lo, z, y, core):
        return (x_hi * 2 + core, (x_lo * 8 + z) * 4 + y)

    def partner(k, j, core):
        return device(*partner_of(k, order_of(k)[j], x_hi, x_lo, z, y), core)

    sibling = device(x_hi, x_lo, z, y, 1 - core)
    across = [device(1 - x_hi, x_lo, z, y, c) for c in range(2)]

    stack = contextlib.ExitStack()

    def phase(name):
        stack.close()
        stack.enter_context(jax.named_scope(name))

    phase("start")
    barrier = pltpu.get_barrier_semaphore()
    peers = [sibling] + across
    for j in range(6):
        peers += [partner(0, j, 0), partner(0, j, 1)]
    peers += [partner(0, 6, core), partner(3, 6, core)]
    for peer in peers:
        pl.semaphore_signal(barrier, inc=1, device_id=peer, device_id_type=MESH)

    loads = [
        pltpu.make_async_copy(src, dst, in_sem.at[i])
        for i, (src, dst) in enumerate(
            (
                (x_hbm, x_ref), (k_hbm, k_ref), (q_hbm, q_ref), (v_hbm, v_ref), (g_hbm, g_ref), (cos_hbm, cos_ref),
                (sin_hbm, sin_ref), (rp_hbm, rp_ref), (gp_hbm, gp_ref), (om_hbm, om_ref), (ni_hbm, ni.at[0]),
            )
        )
    ]
    for load in loads:
        load.start()

    def remote(src, dst, send, receive, peer):
        return pltpu.make_async_remote_copy(
            src_ref=src, dst_ref=dst, send_sem=send, recv_sem=receive, device_id=peer, device_id_type=MESH
        )

    loads[0].wait()

    phase("turn")
    def turn(c, _):
        here = pl.ds(pl.multiple_of(c * 1152, 1152), 1152)
        xt[here, 0:256] = x_ref[:, here].T
        return 0

    lax.fori_loop(0, 4, turn, 0)

    nt = (((1,), (1,)), ((), ()))

    def heads(ch):
        def head(at, _):
            half, x_part = at // 2, at % 2
            h = half * 4 + x_part * 2 + ch
            lanes = pl.ds(pl.multiple_of(h * HD, HD), HD)
            keys = k_ref[:, lanes]
            values = v_ref[:, lanes]
            low = jnp.zeros((128, HD), F32)
            high = jnp.zeros((128, HD), F32)
            for g in range(2):
                wide = pl.ds(pl.multiple_of(h * 256 + g * HD, HD), HD)
                for b in range(2):
                    rows = slice(b * 128, b * 128 + 128)
                    n = (b + 1) * 128
                    qb = q_ref[rows, wide]
                    gb = g_ref[rows, wide]
                    logits = lax.dot_general(keys[:n], qb, nt, preferred_element_type=F32)
                    dprobs = lax.dot_general(values[:n], gb, nt, preferred_element_type=F32)
                    capped = jnp.tanh(logits * (score_scale / soft_cap))
                    unnormed = jnp.exp(soft_cap * capped)
                    key_at = lax.broadcasted_iota(jnp.int32, (n, 128), 0)
                    query_at = lax.broadcasted_iota(jnp.int32, (n, 128), 1) + b * 128
                    unnormed = jnp.where(query_at >= key_at, unnormed, 0.0)
                    inverse = 1.0 / jnp.sum(unnormed, axis=0, keepdims=True)
                    center = jnp.sum(unnormed * dprobs, axis=0, keepdims=True) * inverse
                    dlogits = (
                        unnormed * (dprobs - center) * ((1.0 - capped * capped) * (inverse * score_scale))
                    ).astype(BF16)
                    part = jnp.dot(dlogits, qb, preferred_element_type=F32)
                    low = low + part[:128]
                    if b == 1:
                        high = high + part[128:]
            out_lanes = pl.ds(pl.multiple_of(x_part * HD, HD), HD)
            for b, rotated in ((0, low), (1, high)):
                rows = slice(b * 128, b * 128 + 128)
                plain = rotated * cos_ref[rows, :] + pltpu.roll(rotated, 64, 1) * sin_ref[rows, :]
                kg[half, ch, rows, out_lanes] = plain.astype(BF16)
            return 0

        return head

    def kg_copy(ch):
        return remote(kg.at[1 - core, ch], kg_sib.at[ch], kg_send.at[ch], kg_recv.at[ch], sibling)

    for load in loads[1:8]:
        load.wait()
    phase("attn0")
    lax.fori_loop(0, 2, heads(0), 0)

    phase("barrier")
    pl.semaphore_wait(barrier, len(peers))
    xt_copy = remote(xt.at[:, 0:256], xt.at[:, 256:512], xt_send, xt_recv, sibling)
    xt_copy.start()

    def rep_copy(i, c, slot):
        block = pl.ds(pl.multiple_of(c * 512 + (x_hi if i == 0 else 1 - x_hi) * 256, 256), 256)
        peer = device(x_hi if i == 0 else 1 - x_hi, x_lo, z, y, 1)
        return remote(rp_ref.at[:, block], changes.at[slot, c], rep_send.at[i, c], rep_recv.at[slot, c], peer)

    @pl.when(core == 0)
    def _():
        for c in range(2):
            rep_copy(0, c, 0).start()
            rep_copy(1, c, 2).start()

    @pl.when(core == 1)
    def _():
        for c in range(2):
            rep_copy(1, c, 1).start()

    phase("attn1")
    lax.fori_loop(2, 4, heads(0), 0)
    kg_copy(0).start()
    lax.fori_loop(0, 4, heads(1), 0)
    kg_copy(1).start()
    ni_copy = remote(ni_hbm, ni.at[1], ni_send, ni_recv, sibling)
    ni_copy.start()

    z_hi, z_lo = z // 4, z % 4
    mine = [bits_of(k, x_hi, x_lo, z_hi, z_lo, y) for k in portions]

    def start_of(k, j, flip=False):
        place = 0
        for name in order_of(k)[:j]:
            place = place * 2 + mine[k][name]
        last = mine[k][order_of(k)[j]]
        place = place * 2 + (1 - last if flip else last)
        return place * 2 ** (6 - j)

    def rows_of(s):
        return pl.ds(s * 8, 8)

    def rs_copy(k, j, s):
        n = 2 ** (6 - j)
        return remote(
            grad.at[k, pl.ds(start_of(k, j, True), n), rows_of(s)],
            recv.at[k, pl.ds(128 - 2 * n, n), rows_of(s)],
            rs_send.at[k, j, s],
            rs_recv.at[k, j, s],
            partner(k, j, core),
        )

    def r2_copy(k, s, c):
        return remote(
            grad.at[k, pl.ds(start_of(k, 2, True), 16), rows_of(s)],
            n_recv.at[k, c, :, rows_of(s)],
            r2_send.at[k, s],
            r2_recv.at[c, k, s],
            partner(k, 2, 1),
        )

    def keep_copy(k, s):
        return remote(
            grad.at[k, pl.ds(start_of(k, 2), 16), rows_of(s)],
            n_keep.at[k, :, rows_of(s)],
            keep_send.at[k, s],
            keep_recv.at[k, s],
            sibling,
        )

    for ch in range(2):
        phase(f"grad{ch}")
        if ch == 0:
            xt_copy.wait_recv()
        kg_copy(ch).wait_recv()

        def quarter(c, _, ch=ch):
            rows = pl.ds(pl.multiple_of(c * 1152, 1152), 1152)
            part = jnp.dot(xt[rows, 0:256], kg[core, ch], preferred_element_type=F32) + jnp.dot(
                xt[rows, 256:512], kg_sib[ch], preferred_element_type=F32
            )
            for i in range(16):
                for t_hi in range(2):
                    for k in portions:
                        place = place_of(bits_of(k, t_hi, c // 2, c % 2, i // 4, i % 4), k)
                        for s in range(SUBS):
                            if tile_of(k, s)[0] == ch:
                                row = i * SHARD + tile_of(k, s)[1] * 8
                                piece = part[row : row + 8, t_hi * 128 : t_hi * 128 + 128]
                                grad[k, place, s * 8 : s * 8 + 8] = piece.astype(BF16)
            return 0

        lax.fori_loop(0, 4, quarter, 0)
        for s in range(SUBS):
            for k in portions:
                if tile_of(k, s)[0] == ch:
                    rs_copy(k, 0, s).start()

    for j in range(2):
        n = 2 ** (6 - j)
        for s in range(SUBS):
            phase(f"rs{j}{s}")
            for k in portions:
                rs_copy(k, j, s).wait_recv()
                base = start_of(k, j)

                def add(i, _, k=k, n=n, base=base, s=s):
                    here = pl.ds(base + i * 16, 16)
                    got = recv[k, pl.ds(128 - 2 * n + i * 16, 16), s * 8 : s * 8 + 8]
                    grad[k, here, s * 8 : s * 8 + 8] = grad[k, here, s * 8 : s * 8 + 8] + got
                    return 0

                lax.fori_loop(0, n // 16, add, 0)
                if j == 0:
                    rs_copy(k, 1, s).start()
                else:
                    r2_copy(k, s, core).start()

                    @pl.when(core == 0)
                    def _(k=k, s=s):
                        keep_copy(k, s).start()

    def n_rs_copy(k, j):
        n = 2 ** (6 - j)
        return remote(
            n_sum.at[k, pl.ds(start_of(k, j, True) % 16, n)],
            n_recv2.at[k, pl.ds(16 - 2 * n, n)],
            n_rs_send.at[k, j - 3],
            n_rs_recv.at[k, j - 3],
            partner(k, j, 1),
        )

    def n_ag_copy(k, j):
        n = 2 ** (6 - j)
        here = pl.ds(start_of(k, j) % 16, n)
        return remote(
            n_w.at[k, here], n_w.at[k, here], n_ag_send.at[k, j - 3], n_ag_recv.at[k, j - 3], partner(k, j, 1)
        )

    def a2_copy(k, s, c):
        return remote(
            n_w.at[k, :, c, rows_of(s)],
            weights.at[k, pl.ds(start_of(k, 2), 16), rows_of(s)],
            a2_send.at[c, k, s],
            a2_recv.at[k, s],
            partner(k, 2, c),
        )

    def own_copy(k):
        return remote(
            n_w.at[k, :, 0],
            weights.at[k, pl.ds(start_of(k, 2), 16)],
            own_send.at[k],
            own_recv.at[k],
            sibling,
        )

    def og_copy(i):
        peer = (sibling, across[1], across[0])[i]
        return remote(og.at[x_hi], og.at[x_hi], og_send.at[i], og_recv.at[min(i, 1)], peer)

    @pl.when(core == 1)
    def _():
        for s in range(SUBS):
            phase(f"rs2{s}")
            for k in portions:
                rows = slice(s * 8, s * 8 + 8)
                r2_copy(k, s, 1).wait_recv()
                n_sum[k, :, 1, rows] = grad[k, pl.ds(start_of(k, 2), 16), rows] + n_recv[k, 1, :, rows]
                keep_copy(k, s).wait_recv()
                r2_copy(k, s, 0).wait_recv()
                n_sum[k, :, 0, rows] = n_keep[k, :, rows] + n_recv[k, 0, :, rows]
                if s == SUBS - 1:
                    n_rs_copy(k, 3).start()
        for j in range(3, 7):
            phase(f"rs{j}")
            n = 2 ** (6 - j)
            for k in portions:
                n_rs_copy(k, j).wait_recv()
                here = pl.ds(start_of(k, j) % 16, n)
                n_sum[k, here] = n_sum[k, here] + n_recv2[k, 16 - 2 * n : 16 - n]
                if j < 6:
                    n_rs_copy(k, j + 1).start()

        phase("update")
        for load in loads[8:10]:
            load.wait()
        for c in range(2):
            for slot in range(3):
                rep_copy(1, c, slot).wait_recv()
        for k in portions:
            place = start_of(k, 6) % 16
            for s in range(SUBS):
                ch, tile = tile_of(k, s)
                rows = slice(tile * 8, tile * 8 + 8)
                lanes = slice(ch * 128, ch * 128 + 128)
                for c in range(2):
                    cols = pl.ds(pl.multiple_of(c * 512 + x_hi * 256 + ch * 128, 128), 128)
                    before = gp_ref[rows, cols]
                    moved = before - rp_ref[rows, cols]
                    for slot in range(3):
                        moved = moved + (before - changes[slot, c, rows, lanes])
                    summed = n_sum[k, place, c, s * 8 : s * 8 + 8].astype(F32)
                    outer = (moved + inner_rate * summed) * 0.25
                    og[x_hi, c, rows, lanes] = outer
                    fresh = outer_beta * om_ref[rows, cols] + outer
                    n_w[k, place, c, s * 8 : s * 8 + 8] = (
                        before - outer_rate * (outer + outer_beta * fresh)
                    ).astype(BF16)
            n_ag_copy(k, 6).start()
        for i in range(3):
            og_copy(i).start()
        for j in range(6, 2, -1):
            phase(f"ag{j}")
            for k in portions:
                n_ag_copy(k, j).wait_recv()
                if j > 3:
                    n_ag_copy(k, j - 1).start()
                else:
                    own_copy(k).start()
                    for s in range(SUBS):
                        for c in range(2):
                            a2_copy(k, s, c).start()
        for k in portions:
            weights[k, pl.ds(start_of(k, 2), 16)] = n_w[k, :, 1]

    @pl.when(core == 0)
    def _():
        phase("agown")
        for load in loads[8:10]:
            load.wait()
        for k in portions:
            own_copy(k).wait_recv()

    def ag_copy(k, j, s):
        here = pl.ds(start_of(k, j), 2 ** (6 - j))
        return remote(
            weights.at[k, here, rows_of(s)],
            weights.at[k, here, rows_of(s)],
            ag_send.at[k, j, s],
            ag_recv.at[k, j, s],
            partner(k, j, core),
        )

    for s in range(SUBS):
        phase(f"ag2{s}")
        for k in portions:
            a2_copy(k, s, 0).wait_recv()
            ag_copy(k, 1, s).start()
    for s in range(SUBS):
        phase(f"ag1{s}")
        for k in portions:
            ag_copy(k, 1, s).wait_recv()
            ag_copy(k, 0, s).start()

    def o_copy(ch):
        return remote(o_send.at[ch], o_recv.at[ch], o_ssem.at[ch], o_rsem.at[ch], sibling)

    def project(side, ch):
        total = jnp.zeros((SEQ, 256), F32)
        for part in range(2):
            total = total + jnp.dot(
                ni[side, :, part * 2304 : part * 2304 + 2304],
                w_full[2 * part : 2 * part + 2].reshape(2304, 256),
                preferred_element_type=F32,
            )
        return total.astype(BF16)

    def to_output(half, ch, block):
        for t_hi in range(2):
            lanes = pl.ds(pl.multiple_of(half * 512 + t_hi * 256 + ch * 128, 128), 128)
            nk_ref[:, lanes] = block[:, t_hi * 128 : t_hi * 128 + 128]

    for ch in range(2):
        phase(f"ag0{ch}")
        for s in range(SUBS):
            for k in portions:
                if tile_of(k, s)[0] == ch:
                    ag_copy(k, 0, s).wait_recv()

        phase(f"place{ch}")
        def place_rows(c, _, ch=ch):
            for i in range(16):
                for t_hi in range(2):
                    for k in portions:
                        place = place_of(bits_of(k, t_hi, c // 2, c % 2, i // 4, i % 4), k)
                        for s in range(SUBS):
                            if tile_of(k, s)[0] == ch:
                                row = i * SHARD + tile_of(k, s)[1] * 8
                                w_full[c, row : row + 8, t_hi * 128 : t_hi * 128 + 128] = weights[
                                    k, place, s * 8 : s * 8 + 8
                                ]
            return 0

        lax.fori_loop(0, 4, place_rows, 0)
        if ch == 0:
            loads[10].wait()
            ni_copy.wait_recv()
        phase(f"proj{ch}")
        o_send[ch] = project(1, ch)
        o_copy(ch).start()
        to_output(core, ch, project(0, ch))

    phase("tail")
    @pl.when(core == 0)
    def _():
        og_copy(0).wait_recv()

    og_copy(1).wait_recv()
    for b in range(4):
        lanes = slice(b * 256, b * 256 + 256)
        outer = og[b % 2, b // 2]
        fresh = outer_beta * om_ref[:, lanes] + outer
        nm_ref[:, lanes] = fresh
        np_ref[:, lanes] = gp_ref[:, lanes] - outer_rate * (outer + outer_beta * fresh)
    phase("owait")
    for ch in range(2):
        o_copy(ch).wait_recv()
        to_output(1 - core, ch, o_recv[ch])

    phase("sends")
    for s in range(SUBS):
        for k in portions:
            for j in range(2):
                rs_copy(k, j, s).wait_send()
                ag_copy(k, j, s).wait_send()
            r2_copy(k, s, 0).wait_send()
    for ch in range(2):
        kg_copy(ch).wait_send()
        o_copy(ch).wait_send()
    xt_copy.wait_send()
    ni_copy.wait_send()
    for c in range(2):
        rep_copy(1, c, 0).wait_send()

    @pl.when(core == 0)
    def _():
        for c in range(2):
            rep_copy(0, c, 0).wait_send()
        for k in portions:
            for s in range(SUBS):
                keep_copy(k, s).wait_send()

    @pl.when(core == 1)
    def _():
        for i in range(3):
            og_copy(i).wait_send()
        for k in portions:
            own_copy(k).wait_send()
            for j in range(3, 7):
                n_rs_copy(k, j).wait_send()
                n_ag_copy(k, j).wait_send()
            for s in range(SUBS):
                for c in range(2):
                    a2_copy(k, s, c).wait_send()
    stack.close()


def turning():
    half = HD // 2
    freqs = np.float32(rope_base) ** (-np.arange(half, dtype=np.float32) / np.float32(half))
    angles = np.arange(SEQ, dtype=np.float32)[:, None] * freqs[None, :].astype(np.float32)
    cosine, sine = np.cos(angles), np.sin(angles)
    return (
        np.concatenate([cosine, cosine], axis=1).astype(np.float32),
        np.concatenate([sine, -sine], axis=1).astype(np.float32),
    )


def body(layer_inputs, queries, saved_keys, saved_values, out_grad, global_params, replica_params, outer_momentum, next_inputs):
    cosine, sine = turning()
    vmem = pl.BlockSpec(memory_space=pltpu.VMEM)
    dma = pltpu.SemaphoreType.DMA
    rows = pltpu.VMEM((SHARD, 1024), F32)
    table = pltpu.VMEM((SEQ, HD), F32)
    return pl.pallas_call(
        kernel,
        out_shape=(
            jax.ShapeDtypeStruct((SHARD, 1024), F32),
            jax.ShapeDtypeStruct((SHARD, 1024), F32),
            jax.ShapeDtypeStruct((SEQ, 1024), BF16),
        ),
        in_specs=[pl.BlockSpec(memory_space=pl.ANY)] * 11,
        out_specs=(vmem, vmem, vmem),
        scratch_shapes=[
            pltpu.VMEM((SEQ, D), BF16),
            pltpu.VMEM((SEQ, 2048), BF16),
            pltpu.VMEM((SEQ, 1024), BF16),
            pltpu.VMEM((SEQ, 1024), BF16),
            pltpu.VMEM((SEQ, 2048), BF16),
            rows, rows, rows, table, table,
            pltpu.VMEM((2, SEQ, D), BF16),
            pltpu.VMEM((D, 512), BF16),
            pltpu.VMEM((2, 2, SEQ, 256), BF16),
            pltpu.VMEM((2, SEQ, 256), BF16),
            pltpu.VMEM((PORTIONS, 128, 24, 128), BF16),
            pltpu.VMEM((PORTIONS, 96, 24, 128), BF16),
            pltpu.VMEM((PORTIONS, 16, 24, 128), BF16),
            pltpu.VMEM((PORTIONS, 2, 16, 24, 128), BF16),
            pltpu.VMEM((PORTIONS, 16, 2, 24, 128), BF16),
            pltpu.VMEM((PORTIONS, 16, 2, 24, 128), BF16),
            pltpu.VMEM((PORTIONS, 16, 2, 24, 128), BF16),
            pltpu.VMEM((PORTIONS, 128, 24, 128), BF16),
            pltpu.VMEM((4, 1152, 256), BF16),
            pltpu.VMEM((3, 2, SHARD, 256), F32),
            pltpu.VMEM((2, 2, SHARD, 256), F32),
            pltpu.VMEM((2, SEQ, 256), BF16),
            pltpu.VMEM((2, SEQ, 256), BF16),
            dma((11,)),
            dma((PORTIONS, 2, SUBS)), dma((PORTIONS, 2, SUBS)),
            dma((PORTIONS, SUBS)), dma((2, PORTIONS, SUBS)),
            dma((PORTIONS, SUBS)), dma((PORTIONS, SUBS)),
            dma((PORTIONS, 4)), dma((PORTIONS, 4)),
            dma((PORTIONS, 4)), dma((PORTIONS, 4)),
            dma((2, PORTIONS, SUBS)), dma((PORTIONS, SUBS)),
            dma((PORTIONS,)), dma((PORTIONS,)),
            dma((PORTIONS, 2, SUBS)), dma((PORTIONS, 2, SUBS)),
            dma((2, 2)), dma((3, 2)),
            dma((3,)), dma((2,)),
            dma, dma, dma, dma, dma((2,)), dma((2,)), dma((2,)), dma((2,)),
        ],
        compiler_params=pltpu.CompilerParams(
            collective_id=0, has_side_effects=True, vmem_limit_bytes=60 * 1024 * 1024
        ),
    )(
        layer_inputs, queries, saved_keys, saved_values, out_grad, global_params, replica_params[0],
        outer_momentum, cosine, sine, next_inputs,
    )


def solution(mesh):
    both = ("rep", "fsdp")
    return jax.shard_map(
        body,
        mesh=mesh,
        in_specs=(
            P(both, None), P(both, None), P(both, None), P(both, None), P(both, None),
            P("fsdp", None), P("rep", "fsdp", None), P("fsdp", None), P(both, None),
        ),
        out_specs=(P("fsdp", None), P("fsdp", None), P(both, None)),
        check_vma=False,
    )
```

time: 112 us -> 95.4 us (0.85)
  Pallas kernels: 106 us -> 89.3 us
    pallas_call x1, Pallas kernels: 106 us -> 89.3 us  [body(): pl.pallas_call(kernel, out_shape=(jax.ShapeDtypeStruct((SHARD, 1024), F32...]
where the time goes in v2:
time: 95.4 us; the launch traced here: 95.2 us
  Pallas kernels  89.3 us (94%)
  local copies, waits for them, and re-layouts  5.26 us (6%)
    pallas_call x1, Pallas kernels, body(): pl.pallas_call(kernel, out_shape=(jax.ShapeDtypeStruct((SHARD, 1024), F32...  89.3 us
    unnamed x3, local copies, waits for them, and re-layouts  5.26 us

profile of v2, /device:TPU:1, one launch (start us, length us, event | category | flops | bytes accessed | tf_op | source)
XLA Modules:
  0.0 95.2 jit_solution(11401752015763299498)
XLA Ops:
  0.6 89.3 %shard_map.130 = (f32[72,1024]{1,0:T(8,128)}, f32[72,1024]{1,0:T(8,128)}, bf16[256,1024]{1,0:T(8,128)(2,1)}) custom-call(bf16[256,4608]{1,0:T(8,128)(2,1)} %x_hbm.1, bf16[256,2048]{1,0:T(8,128)(2,1)} %q_hbm.1, bf16[256,1024]{1,0:T(8,128)(2,1)} %k_hbm.1, bf16[256,1024]{1,0:T(8,128)(2,1)} %v_hbm.1, bf16[256,2048]{1,0:T(8,128)(2,1)} %g_hbm.1, ...), custom_call_target="tpu_custom_call" | custom-call | tf_op jit(solution)/shard_map/pallas_call | solution.py:580
  90.0 1.7 %copy.17 = f32[72,1024]{1,0:T(8,128)} copy(f32[72,1024]{1,0:T(8,128)} %get-tuple-element.6) | data formatting | bytes 589824
  91.7 1.7 %copy.18 = f32[72,1024]{1,0:T(8,128)} copy(f32[72,1024]{1,0:T(8,128)} %get-tuple-element.7) | data formatting | bytes 589824
  93.4 1.9 %copy.19 = bf16[256,1024]{1,0:T(8,128)(2,1)} copy(bf16[256,1024]{1,0:T(8,128)(2,1)} %get-tuple-element.8) | data formatting | bytes 1048576

commit v3 on v2

--- a/solution.py
+++ b/solution.py
@@ -88,9 +88,9 @@
     x_hbm, q_hbm, k_hbm, v_hbm, g_hbm, gp_hbm, rp_hbm, om_hbm, cos_hbm, sin_hbm, ni_hbm,
     np_ref, nm_ref, nk_ref,
     x_ref, q_ref, k_ref, v_ref, g_ref, gp_ref, rp_ref, om_ref, cos_ref, sin_ref, ni,
-    xt, kg, kg_sib, grad, recv, n_keep, n_recv, n_sum, n_recv2, n_w, weights, w_full, changes, og, o_send, o_recv,
+    xt, kg, kg_sib, grad, recv, n_keep, n_recv, n_sum, n_recv2, n_w, weights, w_full, changes, og, o_send, o_recv, anchor,
     in_sem, rs_send, rs_recv, r2_send, r2_recv, keep_send, keep_recv, n_rs_send, n_rs_recv, n_ag_send, n_ag_recv,
-    a2_send, a2_recv, own_send, own_recv, ag_send, ag_recv, rep_send, rep_recv, og_send, og_recv,
+    a2_send, a2_recv, own_send, own_recv, ag_send, ag_recv, rep_send, rep_recv, og_send, og_recv, base_send, base_recv,
     ni_send, ni_recv, xt_send, xt_recv, kg_send, kg_recv, o_ssem, o_rsem,
 ):
     rep = lax.axis_index("rep")
@@ -105,6 +105,12 @@
     def partner(k, j, core):
         return device(*partner_of(k, order_of(k)[j], x_hi, x_lo, z, y), core)
 
+    def corner(k):
+        return partner_of(k, order_of(k)[4], *partner_of(k, order_of(k)[3], x_hi, x_lo, z, y))
+
+    def both_of(k, core):
+        return device(*corner(k), core)
+
     sibling = device(x_hi, x_lo, z, y, 1 - core)
     across = [device(1 - x_hi, x_lo, z, y, c) for c in range(2)]
 
@@ -119,7 +125,7 @@
     peers = [sibling] + across
     for j in range(6):
         peers += [partner(0, j, 0), partner(0, j, 1)]
-    peers += [partner(0, 6, core), partner(3, 6, core)]
+    peers += [partner(0, 6, core), partner(3, 6, core)] + [both_of(k, core) for k in portions]
     for peer in peers:
         pl.semaphore_signal(barrier, inc=1, device_id=peer, device_id_type=MESH)
 
@@ -196,11 +202,6 @@
     def kg_copy(ch):
         return remote(kg.at[1 - core, ch], kg_sib.at[ch], kg_send.at[ch], kg_recv.at[ch], sibling)
 
-    for load in loads[1:8]:
-        load.wait()
-    phase("attn0")
-    lax.fori_loop(0, 2, heads(0), 0)
-
     phase("barrier")
     pl.semaphore_wait(barrier, len(peers))
     xt_copy = remote(xt.at[:, 0:256], xt.at[:, 256:512], xt_send, xt_recv, sibling)
@@ -210,6 +211,8 @@
         block = pl.ds(pl.multiple_of(c * 512 + (x_hi if i == 0 else 1 - x_hi) * 256, 256), 256)
         peer = device(x_hi if i == 0 else 1 - x_hi, x_lo, z, y, 1)
         return remote(rp_ref.at[:, block], changes.at[slot, c], rep_send.at[i, c], rep_recv.at[slot, c], peer)
+
+    loads[7].wait()
 
     @pl.when(core == 0)
     def _():
@@ -222,13 +225,14 @@
         for c in range(2):
             rep_copy(1, c, 1).start()
 
-    phase("attn1")
-    lax.fori_loop(2, 4, heads(0), 0)
+    for load in loads[1:7]:
+        load.wait()
+    phase("attn0")
+    lax.fori_loop(0, 4, heads(0), 0)
     kg_copy(0).start()
-    lax.fori_loop(0, 4, heads(1), 0)
-    kg_copy(1).start()
+    phase("attn1a")
+    lax.fori_loop(0, 2, heads(1), 0)
     ni_copy = remote(ni_hbm, ni.at[1], ni_send, ni_recv, sibling)
-    ni_copy.start()
 
     z_hi, z_lo = z // 4, z % 4
     mine = [bits_of(k, x_hi, x_lo, z_hi, z_lo, y) for k in portions]
@@ -254,6 +258,35 @@
             partner(k, j, core),
         )
 
+    def base_copy(side):
+        part = pl.ds(side * 3, 3)
+        return remote(anchor.at[0, part], anchor.at[1, part], base_send.at[side], base_recv.at[side], partner(side * 3, 6, 1))
+
+    def make_base():
+        for load in loads[8:10]:
+            load.wait()
+        for c in range(2):
+            for slot in range(3):
+                rep_copy(1, c, slot).wait_recv()
+        for k in portions:
+            for s in range(SUBS):
+                ch, tile = tile_of(k, s)
+                rows = slice(tile * 8, tile * 8 + 8)
+                lanes = slice(ch * 128, ch * 128 + 128)
+                for c in range(2):
+                    cols = pl.ds(pl.multiple_of(c * 512 + x_hi * 256 + ch * 128, 128), 128)
+                    before = gp_ref[rows, cols]
+                    moved = before - rp_ref[rows, cols]
+                    for slot in range(3):
+                        moved = moved + (before - changes[slot, c, rows, lanes])
+                    outer = moved * 0.25
+                    og[x_hi, c, rows, lanes] = outer
+                    anchor[0, k, c, s * 8 : s * 8 + 8] = before - outer_rate * (
+                        (1.0 + outer_beta) * outer + outer_beta * outer_beta * om_ref[rows, cols]
+                    )
+        for side in range(2):
+            base_copy(side).start()
+
     def r2_copy(k, s, c):
         return remote(
             grad.at[k, pl.ds(start_of(k, 2, True), 16), rows_of(s)],
@@ -273,10 +306,23 @@
         )
 
     for ch in range(2):
+        if ch == 0:
+            phase("base")
+
+            @pl.when(core == 1)
+            def _():
+                make_base()
+
+            phase("xtwait")
+            xt_copy.wait_recv()
+        else:
+            phase("attn1b")
+            lax.fori_loop(2, 4, heads(1), 0)
+            kg_copy(1).start()
+            ni_copy.start()
+            phase("kgwait")
+        kg_copy(ch).wait_recv()
         phase(f"grad{ch}")
-        if ch == 0:
-            xt_copy.wait_recv()
-        kg_copy(ch).wait_recv()
 
         def quarter(c, _, ch=ch):
             rows = pl.ds(pl.multiple_of(c * 1152, 1152), 1152)
@@ -324,22 +370,53 @@
                     def _(k=k, s=s):
                         keep_copy(k, s).start()
 
-    def n_rs_copy(k, j):
-        n = 2 ** (6 - j)
-        return remote(
-            n_sum.at[k, pl.ds(start_of(k, j, True) % 16, n)],
-            n_recv2.at[k, pl.ds(16 - 2 * n, n)],
-            n_rs_send.at[k, j - 3],
-            n_rs_recv.at[k, j - 3],
-            partner(k, j, 1),
-        )
-
-    def n_ag_copy(k, j):
-        n = 2 ** (6 - j)
-        here = pl.ds(start_of(k, j) % 16, n)
-        return remote(
-            n_w.at[k, here], n_w.at[k, here], n_ag_send.at[k, j - 3], n_ag_recv.at[k, j - 3], partner(k, j, 1)
-        )
+    quad = []
+    for k in portions:
+        at = []
+        for chip in (
+            partner_of(k, order_of(k)[3], x_hi, x_lo, z, y),
+            partner_of(k, order_of(k)[4], x_hi, x_lo, z, y),
+            corner(k),
+        ):
+            there = bits_of(k, chip[0], chip[1], chip[2] // 4, chip[2] % 4, chip[3])
+            at.append((device(*chip, 1), (there[order_of(k)[3]] * 2 + there[order_of(k)[4]]) * 4))
+        quad.append(at)
+
+    def n_rs4_copy(k, i):
+        peer, start = quad[k][i]
+        return remote(
+            n_sum.at[k, pl.ds(start, 4)],
+            n_recv2.at[k, pl.ds(4 * i, 4)],
+            n_rs_send.at[k, i],
+            n_rs_recv.at[k, i],
+            peer,
+        )
+
+    def n_ag4_copy(k, i):
+        here = pl.ds(start_of(k, 4) % 16, 4)
+        return remote(n_w.at[k, here], n_w.at[k, here], n_ag_send.at[k, i], n_ag_recv.at[k, i], quad[k][i][0])
+
+    def n_rs5_copy(k):
+        return remote(
+            n_sum.at[k, pl.ds(start_of(k, 5, True) % 16, 2)],
+            n_recv2.at[k, pl.ds(12, 2)],
+            n_rs_send.at[k, 3],
+            n_rs_recv.at[k, 3],
+            partner(k, 5, 1),
+        )
+
+    def n_rs6_copy(k):
+        return remote(
+            n_sum.at[k, pl.ds(start_of(k, 5) % 16, 2)],
+            n_recv2.at[k, pl.ds(14, 2)],
+            n_rs_send.at[k, 4],
+            n_rs_recv.at[k, 4],
+            partner(k, 6, 1),
+        )
+
+    def n_ag5_copy(k):
+        here = pl.ds(start_of(k, 5) % 16, 2)
+        return remote(n_w.at[k, here], n_w.at[k, here], n_ag_send.at[k, 3], n_ag_recv.at[k, 3], partner(k, 5, 1))
 
     def a2_copy(k, s, c):
         return remote(
@@ -375,56 +452,64 @@
                 r2_copy(k, s, 0).wait_recv()
                 n_sum[k, :, 0, rows] = n_keep[k, :, rows] + n_recv[k, 0, :, rows]
                 if s == SUBS - 1:
-                    n_rs_copy(k, 3).start()
-        for j in range(3, 7):
-            phase(f"rs{j}")
-            n = 2 ** (6 - j)
-            for k in portions:
-                n_rs_copy(k, j).wait_recv()
-                here = pl.ds(start_of(k, j) % 16, n)
-                n_sum[k, here] = n_sum[k, here] + n_recv2[k, 16 - 2 * n : 16 - n]
-                if j < 6:
-                    n_rs_copy(k, j + 1).start()
-
-        phase("update")
-        for load in loads[8:10]:
-            load.wait()
-        for c in range(2):
-            for slot in range(3):
-                rep_copy(1, c, slot).wait_recv()
+                    for i in range(3):
+                        n_rs4_copy(k, i).start()
+        phase("rs34")
+        for k in portions:
+            for i in range(3):
+                n_rs4_copy(k, i).wait_recv()
+            here = pl.ds(start_of(k, 4) % 16, 4)
+            total = n_sum[k, here].astype(F32)
+            for i in range(3):
+                total = total + n_recv2[k, 4 * i : 4 * i + 4].astype(F32)
+            n_sum[k, here] = total.astype(BF16)
+            n_rs5_copy(k).start()
+        phase("rs5")
+        for k in portions:
+            n_rs5_copy(k).wait_recv()
+            here = pl.ds(start_of(k, 5) % 16, 2)
+            n_sum[k, here] = n_sum[k, here] + n_recv2[k, 12:14]
+            n_rs6_copy(k).start()
+        phase("rs6")
+        for side in range(2):
+            base_copy(side).wait_recv()
+        for k in portions:
+            n_rs6_copy(k).wait_recv()
+            place = start_of(k, 5) % 16
+            mine_at = mine[k]["zc"]
+            for i in range(2):
+                summed = n_sum[k, place + i].astype(F32) + n_recv2[k, 14 + i].astype(F32)
+                n_w[k, place + i] = (
+                    anchor[(i + mine_at) % 2, k] - (outer_rate * (1.0 + outer_beta) * inner_rate * 0.25) * summed
+                ).astype(BF16)
+            n_ag5_copy(k).start()
+        phase("outer")
         for k in portions:
             place = start_of(k, 6) % 16
+            summed = n_sum[k, place].astype(F32) + n_recv2[k, 14 + mine[k]["zc"]].astype(F32)
             for s in range(SUBS):
                 ch, tile = tile_of(k, s)
                 rows = slice(tile * 8, tile * 8 + 8)
                 lanes = slice(ch * 128, ch * 128 + 128)
                 for c in range(2):
-                    cols = pl.ds(pl.multiple_of(c * 512 + x_hi * 256 + ch * 128, 128), 128)
-                    before = gp_ref[rows, cols]
-                    moved = before - rp_ref[rows, cols]
-                    for slot in range(3):
-                        moved = moved + (before - changes[slot, c, rows, lanes])
-                    summed = n_sum[k, place, c, s * 8 : s * 8 + 8].astype(F32)
-                    outer = (moved + inner_rate * summed) * 0.25
-                    og[x_hi, c, rows, lanes] = outer
-                    fresh = outer_beta * om_ref[rows, cols] + outer
-                    n_w[k, place, c, s * 8 : s * 8 + 8] = (
-                        before - outer_rate * (outer + outer_beta * fresh)
-                    ).astype(BF16)
-            n_ag_copy(k, 6).start()
+                    og[x_hi, c, rows, lanes] = (
+                        og[x_hi, c, rows, lanes] + (inner_rate * 0.25) * summed[c, s * 8 : s * 8 + 8]
+                    )
         for i in range(3):
             og_copy(i).start()
-        for j in range(6, 2, -1):
-            phase(f"ag{j}")
-            for k in portions:
-                n_ag_copy(k, j).wait_recv()
-                if j > 3:
-                    n_ag_copy(k, j - 1).start()
-                else:
-                    own_copy(k).start()
-                    for s in range(SUBS):
-                        for c in range(2):
-                            a2_copy(k, s, c).start()
+        phase("ag5")
+        for k in portions:
+            n_ag5_copy(k).wait_recv()
+            for i in range(3):
+                n_ag4_copy(k, i).start()
+        phase("ag34")
+        for k in portions:
+            for i in range(3):
+                n_ag4_copy(k, i).wait_recv()
+            own_copy(k).start()
+            for s in range(SUBS):
+                for c in range(2):
+                    a2_copy(k, s, c).start()
         for k in portions:
             weights[k, pl.ds(start_of(k, 2), 16)] = n_w[k, :, 1]
 
@@ -460,15 +545,16 @@
     def o_copy(ch):
         return remote(o_send.at[ch], o_recv.at[ch], o_ssem.at[ch], o_rsem.at[ch], sibling)
 
-    def project(side, ch):
-        total = jnp.zeros((SEQ, 256), F32)
-        for part in range(2):
-            total = total + jnp.dot(
-                ni[side, :, part * 2304 : part * 2304 + 2304],
+    def project():
+        halves = [
+            jnp.dot(
+                ni[:, :, part * 2304 : part * 2304 + 2304].reshape(2 * SEQ, 2304),
                 w_full[2 * part : 2 * part + 2].reshape(2304, 256),
                 preferred_element_type=F32,
             )
-        return total.astype(BF16)
+            for part in range(2)
+        ]
+        return (halves[0] + halves[1]).astype(BF16)
 
     def to_output(half, ch, block):
         for t_hi in range(2):
@@ -501,9 +587,10 @@
             loads[10].wait()
             ni_copy.wait_recv()
         phase(f"proj{ch}")
-        o_send[ch] = project(1, ch)
+        block = project()
+        o_send[ch] = block[SEQ:]
         o_copy(ch).start()
-        to_output(core, ch, project(0, ch))
+        to_output(core, ch, block[:SEQ])
 
     phase("tail")
     @pl.when(core == 0)
@@ -549,15 +636,31 @@
     def _():
         for i in range(3):
             og_copy(i).wait_send()
+        for side in range(2):
+            base_copy(side).wait_send()
         for k in portions:
             own_copy(k).wait_send()
-            for j in range(3, 7):
-                n_rs_copy(k, j).wait_send()
-                n_ag_copy(k, j).wait_send()
+            for i in range(3):
+                n_rs4_copy(k, i).wait_send()
+                n_ag4_copy(k, i).wait_send()
+            n_rs5_copy(k).wait_send()
+            n_rs6_copy(k).wait_send()
+            n_ag5_copy(k).wait_send()
             for s in range(SUBS):
                 for c in range(2):
                     a2_copy(k, s, c).wait_send()
     stack.close()
+
+
+def store(np_ref, nm_ref, nk_ref, np_hbm, nm_hbm, nk_hbm, sems):
+    copies = [
+        pltpu.make_async_copy(src, dst, sems.at[i])
+        for i, (src, dst) in enumerate(((nk_ref, nk_hbm), (np_ref, np_hbm), (nm_ref, nm_hbm)))
+    ]
+    for copy in copies:
+        copy.start()
+    for copy in copies:
+        copy.wait()
 
 
 def turning():
@@ -577,14 +680,14 @@
     dma = pltpu.SemaphoreType.DMA
     rows = pltpu.VMEM((SHARD, 1024), F32)
     table = pltpu.VMEM((SEQ, HD), F32)
-    return pl.pallas_call(
+    results = pl.pallas_call(
         kernel,
         out_shape=(
-            jax.ShapeDtypeStruct((SHARD, 1024), F32),
-            jax.ShapeDtypeStruct((SHARD, 1024), F32),
-            jax.ShapeDtypeStruct((SEQ, 1024), BF16),
+            pltpu.VMEM((SHARD, 1024), F32),
+            pltpu.VMEM((SHARD, 1024), F32),
+            pltpu.VMEM((SEQ, 1024), BF16),
         ),
-        in_specs=[pl.BlockSpec(memory_space=pl.ANY)] * 11,
+        in_specs=[pl.BlockSpec(memory_space=pltpu.HBM)] * 11,
         out_specs=(vmem, vmem, vmem),
         scratch_shapes=[
             pltpu.VMEM((SEQ, D), BF16),
@@ -610,26 +713,39 @@
             pltpu.VMEM((2, 2, SHARD, 256), F32),
             pltpu.VMEM((2, SEQ, 256), BF16),
             pltpu.VMEM((2, SEQ, 256), BF16),
+            pltpu.VMEM((2, PORTIONS, 2, 24, 128), F32),
             dma((11,)),
             dma((PORTIONS, 2, SUBS)), dma((PORTIONS, 2, SUBS)),
             dma((PORTIONS, SUBS)), dma((2, PORTIONS, SUBS)),
             dma((PORTIONS, SUBS)), dma((PORTIONS, SUBS)),
-            dma((PORTIONS, 4)), dma((PORTIONS, 4)),
+            dma((PORTIONS, 5)), dma((PORTIONS, 5)),
             dma((PORTIONS, 4)), dma((PORTIONS, 4)),
             dma((2, PORTIONS, SUBS)), dma((PORTIONS, SUBS)),
             dma((PORTIONS,)), dma((PORTIONS,)),
             dma((PORTIONS, 2, SUBS)), dma((PORTIONS, 2, SUBS)),
             dma((2, 2)), dma((3, 2)),
-            dma((3,)), dma((2,)),
+            dma((3,)), dma((2,)), dma((2,)), dma((2,)),
             dma, dma, dma, dma, dma((2,)), dma((2,)), dma((2,)), dma((2,)),
         ],
         compiler_params=pltpu.CompilerParams(
-            collective_id=0, has_side_effects=True, vmem_limit_bytes=60 * 1024 * 1024
+            collective_id=0, has_side_effects=True, vmem_limit_bytes=54 * 1024 * 1024
         ),
     )(
         layer_inputs, queries, saved_keys, saved_values, out_grad, global_params, replica_params[0],
         outer_momentum, cosine, sine, next_inputs,
     )
+    return pl.pallas_call(
+        store,
+        out_shape=(
+            jax.ShapeDtypeStruct((SHARD, 1024), F32),
+            jax.ShapeDtypeStruct((SHARD, 1024), F32),
+            jax.ShapeDtypeStruct((SEQ, 1024), BF16),
+        ),
+        in_specs=(vmem, vmem, vmem),
+        out_specs=[pl.BlockSpec(memory_space=pltpu.HBM)] * 3,
+        scratch_shapes=[dma((3,))],
+        compiler_params=pltpu.CompilerParams(vmem_limit_bytes=4 * 1024 * 1024),
+    )(*results)
 
 
 def solution(mesh):

time: 95.4 us -> 87.4 us (0.916)
  local copies, waits for them, and re-layouts: 5.26 us -> 0 us
  Pallas kernels: 89.3 us -> 86.7 us
    unnamed x3 -> x0, local copies, waits for them, and re-layouts: 5.26 us -> none
    pallas_call x1 -> x2, Pallas kernels: 89.3 us -> 86.7 us  [the longest x1 85.7 us: body(): pl.pallas_call(kernel, out_shape=(pltpu.VMEM((SHARD, 1024), F32), pltpu.V...]
where the time goes in v3:
time: 87.4 us; the launch traced here: 87.3 us
  Pallas kernels  86.7 us (99%)
    pallas_call x1, Pallas kernels, body(): pl.pallas_call(kernel, out_shape=(pltpu.VMEM((SHARD, 1024), F32), pltpu.V...  85.7 us

profile of v3, /device:TPU:1, one launch (start us, length us, event | category | flops | bytes accessed | tf_op | source)
XLA Modules:
  0.0 87.3 jit_solution(17999407043753545102)
XLA Ops:
  0.6 85.7 %shard_map.130 = (f32[72,1024]{1,0:T(8,128)S(1)}, f32[72,1024]{1,0:T(8,128)S(1)}, bf16[256,1024]{1,0:T(8,128)(2,1)S(1)}) custom-call(bf16[256,4608]{1,0:T(8,128)(2,1)} %x_hbm.1, bf16[256,2048]{1,0:T(8,128)(2,1)} %q_hbm.1, bf16[256,1024]{1,0:T(8,128)(2,1)} %k_hbm.1, bf16[256,1024]{1,0:T(8,128)(2,1)} %v_hbm.1, bf16[256,2048]{1,0:T(8,128)(2,1)} %g_hbm.1, ...), custom_call_target="tpu_custom_call" | custom-call | tf_op jit(solution)/shard_map/pallas_call | solution.py:683
  86.3 1.0 %shard_map.131 = (f32[72,1024]{1,0:T(8,128)}, f32[72,1024]{1,0:T(8,128)}, bf16[256,1024]{1,0:T(8,128)(2,1)}) custom-call(f32[72,1024]{1,0:T(8,128)S(1)} %get-tuple-element.6.np_ref, f32[72,1024]{1,0:T(8,128)S(1)} %get-tuple-element.7.nm_ref, bf16[256,1024]{1,0:T(8,128)(2,1)S(1)} %get-tuple-element.8.nk_ref), custom_call_target="tpu_custom_call" | custom-call | tf_op jit(solution)/shard_map/pallas_call | solution.py:737
